TPU v7x, 32 devices: a whole 2x2x4 slice. The times are simulated.
32 devices in a mesh: grp: 2 (over x), slab: 16 (over z, y, core).
Axes of the slice: x: 2, y: 2, z: 4, core: 2. Of those that a mesh axis runs over, the one named last changes fastest.
Arguments:
- volume: bfloat16 [64, 1024, 1024], P(('grp', 'slab')), parts along dimension 0, may hold values from -60 to 60
- plane_shift: int32 [4, 32], P('grp', 'slab'), parts along dimension 0, may hold values from -64 to 64
- plane_weight: float32 [4, 32], P('grp', 'slab'), parts along dimension 0, may hold values from 0 to 1
- column_left: int32 [4, 1024], P('grp'), parts along dimension 0, may hold values from 0 to 1022
- column_weight: float32 [4, 1024], P('grp'), parts along dimension 0, may hold values from 0 to 1
- window_center: int32 [4, 2], P('grp'), parts along dimension 0, may hold values from -200 to 199
- tilt_owner: int32 [32], P('grp'), parts along dimension 0, may hold values from 0 to 15, each once
- reference_band: float32 [32, 2, 128, 128], P(('grp', 'slab')), parts along dimension 0, may hold values from -6 to 6
Outputs:
- correlation: float32 [4, 16, 128], P('grp', 'slab'), parts along dimension 0
- peaks: float32 [4], P('grp'), parts along dimension 0
There are 2 independent parts, one for each index of `grp`. A program takes and returns all parts, laid end to end along the dimension named above; each array names one. Nothing has to cross between parts.
Inputs may be any that keep to these rules, and one draw needn't show every extreme that they name: `tilt_owner`: the first 2 entries name the owners of the tilts, one slab index each.
All inputs are finite; a program needn't handle non-finite values.
Results may differ from a plain program's by a relative error of at most 0.0003.
Values sent between devices are 32-bit elements; how exact they have to be, the bound alone decides.
A program may use at most 128 MiB of HBM per device.

v0:
```python
import math
import jax
import jax.numpy as jnp
from jax import lax
from jax.sharding import PartitionSpec as P

Y = 1024
X = 1024
BAND = 128
WIN_COLS = 128
TILTS = 2
WIN_ROWS_DEV = 1


def from_root(value, axis, source):
    kept = jnp.where(lax.axis_index(axis) == source, value, 0).astype(value.dtype)
    return lax.psum(kept, axis)


def phase_pair(left_ints, right_ints, length):
    product = left_ints[:, None] * right_ints[None, :] % length
    angle = product.astype(jnp.float32) * (2.0 * math.pi / length)
    return (jnp.cos(angle), jnp.sin(angle))


def matmul(first, second):
    return jnp.dot(
        first, second, precision=lax.Precision.HIGHEST, preferred_element_type=jnp.float32
    )


def reproject(volume, shifts, weights, left_cols, right_share, row_count):
    grid_width = volume.shape[2]
    margin = grid_width // 16 + 1
    padded_all = jnp.pad(volume, ((0, 0), (0, 0), (margin, margin)))
    summed = jnp.zeros((row_count, grid_width), jnp.float32)
    for plane_no in range(volume.shape[0]):
        padded = padded_all[plane_no]
        near_cells = lax.dynamic_slice_in_dim(
            padded, margin - shifts[plane_no], grid_width, 1
        ).astype(jnp.float32)
        far_cells = lax.dynamic_slice_in_dim(
            padded, margin - shifts[plane_no] - 1, grid_width, 1
        ).astype(jnp.float32)
        summed = summed + (1.0 - weights[plane_no]) * near_cells + weights[plane_no] * far_cells
    left_values = jnp.take(summed, left_cols, axis=1)
    right_values = jnp.take(summed, left_cols + 1, axis=1)
    return (1.0 - right_share) * left_values + right_share * right_values


def band_part(projected):
    row_count, grid_width = projected.shape
    freq_cols = jnp.arange(BAND, dtype=jnp.int32)
    freq_rows = freq_cols - BAND // 2
    col_cos, col_sin = phase_pair(jnp.arange(grid_width, dtype=jnp.int32), freq_cols, grid_width)
    real_half = matmul(projected, col_cos)
    imag_half = -matmul(projected, col_sin)
    row_ids = jnp.arange(row_count, dtype=jnp.int32)
    row_cos, row_sin = phase_pair(freq_rows, row_ids, Y)
    spec_real = matmul(row_cos, real_half) + matmul(row_sin, imag_half)
    spec_imag = matmul(row_cos, imag_half) - matmul(row_sin, real_half)
    return jnp.stack([spec_real, spec_imag])


def correlate(spectrum, owned, center, row_ids, total_rows):
    spec_real, spec_imag = (spectrum[0], spectrum[1])
    ref_real, ref_imag = (owned[0], owned[1])
    cross_real = spec_real * ref_real + spec_imag * ref_imag
    cross_imag = spec_imag * ref_real - spec_real * ref_imag
    energy_spec = jnp.mean(spec_real * spec_real + spec_imag * spec_imag) + 1e-06
    energy_ref = jnp.mean(ref_real * ref_real + ref_imag * ref_imag) + 1e-06
    freq_cols = jnp.arange(BAND, dtype=jnp.int32)
    freq_rows = freq_cols - BAND // 2
    offsets_y = center[0] + row_ids - total_rows // 2
    offsets_x = center[1] + jnp.arange(WIN_COLS, dtype=jnp.int32) - WIN_COLS // 2
    row_cos, row_sin = phase_pair(offsets_y, freq_rows, Y)
    col_cos, col_sin = phase_pair(freq_cols, offsets_x, X)
    half_real = matmul(row_cos, cross_real) - matmul(row_sin, cross_imag)
    half_imag = matmul(row_cos, cross_imag) + matmul(row_sin, cross_real)
    return (matmul(half_real, col_cos) - matmul(half_imag, col_sin)) / (
        BAND * jnp.sqrt(energy_spec * energy_ref)
    )


def per_device(
    volume,
    plane_shift,
    plane_weight,
    column_left,
    column_weight,
    window_center,
    tilt_owner,
    reference_band,
):
    devices = lax.axis_size("slab")
    position = lax.axis_index("slab")
    partials = []
    for which in range(TILTS):

        def rows_term(first_row, row_count, which=which):
            return reproject(
                volume,
                plane_shift[which],
                plane_weight[which],
                column_left[which],
                column_weight[which],
                row_count,
            )

        partials.append(band_part(rows_term(0, Y)))
    stacked = jnp.stack(partials)
    mine = reference_band[0]
    spectra = lax.psum(stacked, "slab")
    references = jnp.stack([from_root(mine, "slab", tilt_owner[which]) for which in range(TILTS)])
    total_rows = WIN_ROWS_DEV * devices
    outputs = []
    maxima = []
    row_ids = position * WIN_ROWS_DEV + jnp.arange(WIN_ROWS_DEV, dtype=jnp.int32)
    for which in range(TILTS):
        corr = correlate(
            spectra[which], references[which], window_center[which], row_ids, total_rows
        )
        outputs.append(corr)
        maxima.append(jnp.max(corr))
    peaks = lax.pmax(jnp.stack(maxima), "slab")
    return (jnp.stack(outputs), peaks)


def solution(mesh):
    placed = (
        P(("grp", "slab"), None, None),
        P("grp", "slab"),
        P("grp", "slab"),
        P("grp", None),
        P("grp", None),
        P("grp", None),
        P("grp"),
        P(("grp", "slab"), None, None, None),
    )
    return jax.shard_map(
        per_device,
        mesh=mesh,
        in_specs=placed,
        out_specs=(P("grp", "slab", None), P("grp")),
        check_vma=False,
    )
```

profile of v0, /device:TPU:0, one launch (start us, length us, event | category | flops | bytes accessed | tf_op | source)
XLA Modules:
  0.0 311.6 jit_solution(11527147601551082680)
XLA Ops:
  24.0 6.2 %copy.10 = bf16[2,1024,1024]{1,2,0:T(8,128)(2,1)} copy(bf16[2,1024,1024]{2,1,0:T(8,128)(2,1)} %param.10) | data formatting | bytes 8388608 | tf_op args[0]
  30.2 5.0 %pad_slice_fusion.1 = (bf16[1,1024,1154]{1,2,0:T(8,128)(2,1)S(1)}, bf16[1,1024,1154]{1,2,0:T(8,128)(2,1)}) fusion(bf16[2,1024,1024]{1,2,0:T(8,128)(2,1)} %copy.10), kind=kLoop, calls=%fused_computation.5 | loop fusion | bytes 8921088 | tf_op jit(solution)/shard_map/slice | solution.py:38
  35.2 12.6 %add_bitcast_fusion.1 = (f32[1024,1024]{0,1:T(8,128)}, f32[1024,1024]{0,1:T(8,128)}) fusion(bf16[1,1024,1154]{1,2,0:T(8,128)(2,1)} %get-tuple-element.11, s32[]{:T(128)S(6)} %select_n.127, f32[]{:T(128)} %bitcast.11, s32[]{:T(128)S(6)} %select_n.126, f32[]{:T(128)S(6)} %sub.140, bf16[1,1024,1154]{1,2,0:T(8,128)(2,1)S(1)} %get-tuple-element.10, ...), kind=kLoop, calls=%fused_computation.13 | loop fusion | flops 23068672 | bytes 25165888 | tf_op jit(solution)/shard_map/add | solution.py:45
  47.8 8.6 %gather_fusion.2 = f32[1024,1024]{1,0:T(8,128)} fusion(f32[1024,1024]{0,1:T(8,128)} %get-tuple-element.9, s32[1024]{0:T(1024)S(1)} %get-tuple-element.34), kind=kCustom, calls=%fused_computation.2.clone | custom fusion | bytes 8392704 | tf_op jit(solution)/shard_map/jit(_take)/gather | solution.py:46
  56.4 8.6 %gather_fusion.3 = f32[1024,1024]{1,0:T(8,128)} fusion(f32[1024,1024]{0,1:T(8,128)} %get-tuple-element.9, s32[1024]{0:T(1024)S(1)} %get-tuple-element.35), kind=kCustom, calls=%fused_computation.3.clone | custom fusion | bytes 8392704 | tf_op jit(solution)/shard_map/jit(_take)/gather | solution.py:47
  65.0 4.4 %fusion = f32[1024,1024]{0,1:T(8,128)S(1)} fusion(f32[1024,1024]{1,0:T(8,128)} %gather_fusion.3, f32[1024,1024]{1,0:T(8,128)} %gather_fusion.2, f32[1024]{0:T(1024)S(1)} %bitcast.250, f32[1024]{0:T(1024)S(1)} %bitcast.249, pred[1024]{0:T(1024)(128)(4,1)S(1)} %get-tuple-element.33, pred[1024]{0:T(1024)(128)(4,1)S(1)} %get-tuple-element.32), kind=kLoop, calls=%fused_computation.7 | loop fusion | flops 5242880 | bytes 12593152 | tf_op jit(solution)/shard_map/add | solution.py:48
  69.4 8.5 %fusion.32 = f32[1024,128]{1,0:T(8,128)S(1)} fusion(f32[1024,1024]{0,1:T(8,128)S(1)} %fusion), kind=kOutput, calls=%fused_computation.69 | convolution fusion | flops 1612447744 | bytes 4718592 | tf_op jit(solution)/shard_map/dot_general | solution.py:27
  77.9 21.3 %convolution_negate_fusion = f32[1024,128]{1,0:T(8,128)S(1)} fusion(f32[1024,1024]{0,1:T(8,128)S(1)} %fusion), kind=kOutput, calls=%fused_computation.14 | convolution fusion | flops 1612578816 | bytes 4718592 | tf_op jit(solution)/shard_map/dot_general | solution.py:27
  99.2 8.6 %gather_fusion = f32[1024,1024]{1,0:T(8,128)} fusion(f32[1024,1024]{0,1:T(8,128)} %get-tuple-element.8, s32[1024]{0:T(1024)S(1)} %get-tuple-element.30), kind=kCustom, calls=%fused_computation.clone | custom fusion | bytes 8392704 | tf_op jit(solution)/shard_map/jit(_take)/gather | solution.py:46
  107.8 8.6 %gather_fusion.1 = f32[1024,1024]{1,0:T(8,128)} fusion(f32[1024,1024]{0,1:T(8,128)} %get-tuple-element.8, s32[1024]{0:T(1024)S(1)} %get-tuple-element.31), kind=kCustom, calls=%fused_computation.1.clone | custom fusion | bytes 8392704 | tf_op jit(solution)/shard_map/jit(_take)/gather | solution.py:47
  116.4 4.0 %fusion.1 = f32[1024,1024]{0,1:T(8,128)S(1)} fusion(f32[1024,1024]{1,0:T(8,128)} %gather_fusion.1, f32[1024,1024]{1,0:T(8,128)} %gather_fusion, f32[1024]{0:T(1024)S(1)} %bitcast.248, f32[1024]{0:T(1024)S(1)} %bitcast.247, pred[1024]{0:T(1024)(128)(4,1)S(1)} %get-tuple-element.29, pred[1024]{0:T(1024)(128)(4,1)S(1)} %get-tuple-element.28), kind=kLoop, calls=%fused_computation.10 | loop fusion | flops 5242880 | bytes 12593152 | tf_op jit(solution)/shard_map/add | solution.py:48
  120.4 8.5 %fusion.34 = f32[1024,128]{1,0:T(8,128)S(1)} fusion(f32[1024,1024]{0,1:T(8,128)S(1)} %fusion.1), kind=kOutput, calls=%fused_computation.70 | convolution fusion | flops 1612447744 | bytes 4718592 | tf_op jit(solution)/shard_map/dot_general | solution.py:27
  128.9 8.9 %convolution_negate_fusion.1 = f32[1024,128]{1,0:T(8,128)S(1)} fusion(f32[1024,1024]{0,1:T(8,128)S(1)} %fusion.1), kind=kOutput, calls=%fused_computation.15 | convolution fusion | flops 1612578816 | bytes 4718592 | tf_op jit(solution)/shard_map/dot_general | solution.py:27
  137.9 3.0 fusion.42
  140.9 3.0 fusion.40
  143.9 3.0 fusion.3
  146.9 3.0 fusion.2
  149.9 3.0 fusion.46
  152.9 3.2 %fusion.44 = f32[128,128]{1,0:T(8,128)S(1)} fusion(f32[1024,128]{1,0:T(8,128)S(1)} %convolution_negate_fusion.1, s32[128]{0:T(128)S(1)} %iota_add_fusion), kind=kOutput, calls=%fused_computation.75 | convolution fusion | flops 203161600 | bytes 590336 | tf_op jit(solution)/shard_map/dot_general | solution.py:27
  156.1 3.0 fusion.5
  159.1 3.0 fusion.4
  168.7 91.1 %all-reduce.4.cloned.1.call-done = (f32[2,2,128,128]{3,2,1,0:T(8,128)}, f32[2,128,128]{2,1,0:T(8,128)}, f32[2,128,128]{2,1,0:T(8,128)}) async-done(((f32[2,2,128,128]{3,2,1,0:T(8,128)}, f32[2,128,128]{2,1,0:T(8,128)}, f32[2,128,128]{2,1,0:T(8,128)}), (f32[2,2,128,128]{3,2,1,0:T(8,128)}, f32[2,128,128]{2,1,0:T(8,128)}, f32[2,128,128]{2,1,0:T(8,128)})) %all-reduce.4.cloned.1.call-update) | async-done | bytes 524304 | tf_op jit(solution)/shard_map/psum | solution.py:113
  259.8 1.7 multiply_subtract_fusion.1
  271.8 32.3 %pmax.7 = f32[2]{0:T(128)} all-reduce(f32[2]{0:T(128)S(1)} %pad_maximum_fusion.2), channel_id=1, replica_groups=mesh['grp'=2,'slab'=16] {'slab'}, use_global_device_ids=true, to_apply=%region_9.11 | all-reduce | flops 2 | bytes 16 | tf_op jit(solution)/shard_map/pmax | solution.py:125
  (41 shorter events, 15.9 us)
Async XLA Ops:
  7.2 252.6 %all-reduce.4.cloned.1.call-start = ((), (), s32[]{:S(2)}) async-start(), calls=%async_computation | async-start | bytes 1048576 | tf_op jit(solution)/shard_map/psum | solution.py:113
  56.4 8.6 %copy-start.1 = (f32[2,1024]{1,0:T(2,128)S(1)}, f32[2,1024]{1,0:T(2,128)}, u32[]{:S(2)}) copy-start(f32[2,1024]{1,0:T(2,128)} %param.14) | copy-start | bytes 24580
  149.9 12.2 %copy-start.3 = (s32[16]{0:T(128)S(1)}, s32[16]{0:T(128)}, u32[]{:S(2)}) copy-start(s32[16]{0:T(128)} %param.16) | copy-start | bytes 196
  152.9 11.8 %copy-start = (f32[1,2,128,128]{3,2,1,0:T(8,128)S(1)}, f32[1,2,128,128]{3,2,1,0:T(8,128)}, u32[]{:S(2)}) copy-start(f32[1,2,128,128]{3,2,1,0:T(8,128)} %param.17) | copy-start | bytes 393220
  152.9 12.6 %copy-start.2 = (s32[2,2]{1,0:T(2,128)S(1)}, s32[2,2]{1,0:T(2,128)}, u32[]{:S(2)}) copy-start(s32[2,2]{1,0:T(2,128)} %param.15) | copy-start | bytes 52
Sparse Core Ops, SparseCore 0:
  165.6 94.1 all-reduce.3
where the time goes:
time: 318 us; the launch traced here: 312 us
  waiting for transfers between devices  91.1 us (29%)
  matrix products  75.9 us (24%)
  local copies, waits for them, and re-layouts  50.6 us (16%)
  between operations  32.7 us (10%)
  blocking collectives  32.3 us (10%)
  other arithmetic  29 us (9%)
    psum x1, waiting for transfers between devices, per_device(): spectra = lax.psum(stacked, 'slab')  91.1 us
    dot_general x24, matrix products, matmul(): jnp.dot(first, second, precision=lax.Precision.HIGHEST, preferred_element...  75.9 us
    pmax x1, blocking collectives, per_device(): peaks = lax.pmax(jnp.stack(maxima), 'slab')  32.3 us
    gather x2, local copies, waits for them, and re-layouts, reproject(): right_values = jnp.take(summed, left_cols + 1, axis=1)  17.2 us
    gather x2, local copies, waits for them, and re-layouts, reproject(): left_values = jnp.take(summed, left_cols, axis=1)  17.2 us
    add x1, other arithmetic, reproject(): summed + (1.0 - weights[plane_no]) * near_cells  12.6 us
    add x2, other arithmetic, reproject(): return (1.0 - right_share) * left_values + right_share * right_values  8.41 us
  transfers between devices with their start and end apart: 1, of which 1 were waited for; matrix products, arithmetic and copies ran while one was open for 1% of the time, Pallas kernels for 0%

commit v1 on v0

--- a/solution.py
+++ b/solution.py
@@ -110,7 +110,7 @@
         partials.append(band_part(rows_term(0, Y)))
     stacked = jnp.stack(partials)
     mine = reference_band[0]
-    spectra = lax.psum(stacked, "slab")
+    spectra = jnp.sum(lax.all_gather(stacked, "slab"), axis=0)
     references = jnp.stack([from_root(mine, "slab", tilt_owner[which]) for which in range(TILTS)])
     total_rows = WIN_ROWS_DEV * devices
     outputs = []

time: 318 us -> 366 us (1.15)
  waiting for transfers between devices: 91.1 us -> 137 us
    all_gather x0 -> x1, waiting for transfers between devices: none -> 47.5 us  [per_device(): spectra = jnp.sum(lax.all_gather(stacked, 'slab'), axis=0)]
  transfers between devices with their start and end apart: 1 -> 2, of which waited for: 1 -> 2; matrix products, arithmetic and copies ran while one was open for 1% -> 2% of each run, Pallas kernels for 0% -> 0%
where the time goes in v1:
time: 366 us; the launch traced here: 360 us
  waiting for transfers between devices  137 us (37%)
  matrix products  75.9 us (21%)
  local copies, waits for them, and re-layouts  50.6 us (14%)
  between operations  32.7 us (9%)
  blocking collectives  32.4 us (9%)
  other arithmetic  31.2 us (9%)
    psum x1, waiting for transfers between devices, from_root(): return lax.psum(kept, axis)  89.5 us
    dot_general x24, matrix products, matmul(): jnp.dot(first, second, precision=lax.Precision.HIGHEST, preferred_element...  75.9 us
    all_gather x1, waiting for transfers between devices, per_device(): spectra = jnp.sum(lax.all_gather(stacked, 'slab'), axis=0)  47.5 us
    pmax x1, blocking collectives, per_device(): peaks = lax.pmax(jnp.stack(maxima), 'slab')  32.4 us
    gather x2, local copies, waits for them, and re-layouts, reproject(): right_values = jnp.take(summed, left_cols + 1, axis=1)  17.2 us
    gather x2, local copies, waits for them, and re-layouts, reproject(): left_values = jnp.take(summed, left_cols, axis=1)  17.2 us
    add x1, other arithmetic, reproject(): summed + (1.0 - weights[plane_no]) * near_cells  12.6 us
    add x2, other arithmetic, reproject(): return (1.0 - right_share) * left_values + right_share * right_values  8.41 us
  transfers between devices with their start and end apart: 2, of which 2 were waited for; matrix products, arithmetic and copies ran while one was open for 2% of the time, Pallas kernels for 0%

profile of v1, /device:TPU:0, one launch (start us, length us, event | category | flops | bytes accessed | tf_op | source)
XLA Modules:
  0.0 359.8 jit_solution(15411603438826924273)
XLA Ops:
  24.0 6.2 %copy.11 = bf16[2,1024,1024]{1,2,0:T(8,128)(2,1)} copy(bf16[2,1024,1024]{2,1,0:T(8,128)(2,1)} %param.10) | data formatting | bytes 8388608 | tf_op args[0]
  30.2 5.0 %pad_slice_fusion.1 = (bf16[1,1024,1154]{1,2,0:T(8,128)(2,1)S(1)}, bf16[1,1024,1154]{1,2,0:T(8,128)(2,1)}) fusion(bf16[2,1024,1024]{1,2,0:T(8,128)(2,1)} %copy.11), kind=kLoop, calls=%fused_computation.5 | loop fusion | bytes 8921088 | tf_op jit(solution)/shard_map/slice | solution.py:38
  35.2 12.6 %add_bitcast_fusion.1 = (f32[1024,1024]{0,1:T(8,128)}, f32[1024,1024]{0,1:T(8,128)}) fusion(bf16[1,1024,1154]{1,2,0:T(8,128)(2,1)} %get-tuple-element.10, s32[]{:T(128)S(6)} %select_n.127, f32[]{:T(128)} %bitcast.11, s32[]{:T(128)S(6)} %select_n.126, f32[]{:T(128)S(6)} %sub.140, bf16[1,1024,1154]{1,2,0:T(8,128)(2,1)S(1)} %get-tuple-element.9, ...), kind=kLoop, calls=%fused_computation.13 | loop fusion | flops 23068672 | bytes 25165888 | tf_op jit(solution)/shard_map/add | solution.py:45
  47.8 8.6 %gather_fusion.2 = f32[1024,1024]{1,0:T(8,128)} fusion(f32[1024,1024]{0,1:T(8,128)} %get-tuple-element.8, s32[1024]{0:T(1024)S(1)} %get-tuple-element.33), kind=kCustom, calls=%fused_computation.2.clone | custom fusion | bytes 8392704 | tf_op jit(solution)/shard_map/jit(_take)/gather | solution.py:46
  56.4 8.6 %gather_fusion.3 = f32[1024,1024]{1,0:T(8,128)} fusion(f32[1024,1024]{0,1:T(8,128)} %get-tuple-element.8, s32[1024]{0:T(1024)S(1)} %get-tuple-element.34), kind=kCustom, calls=%fused_computation.3.clone | custom fusion | bytes 8392704 | tf_op jit(solution)/shard_map/jit(_take)/gather | solution.py:47
  65.0 4.4 %fusion = f32[1024,1024]{0,1:T(8,128)S(1)} fusion(f32[1024,1024]{1,0:T(8,128)} %gather_fusion.3, f32[1024,1024]{1,0:T(8,128)} %gather_fusion.2, f32[1024]{0:T(1024)S(1)} %bitcast.252, f32[1024]{0:T(1024)S(1)} %bitcast.251, pred[1024]{0:T(1024)(128)(4,1)S(1)} %get-tuple-element.32, pred[1024]{0:T(1024)(128)(4,1)S(1)} %get-tuple-element.31), kind=kLoop, calls=%fused_computation.7 | loop fusion | flops 5242880 | bytes 12593152 | tf_op jit(solution)/shard_map/add | solution.py:48
  69.4 8.5 %fusion.32 = f32[1024,128]{1,0:T(8,128)S(1)} fusion(f32[1024,1024]{0,1:T(8,128)S(1)} %fusion), kind=kOutput, calls=%fused_computation.69 | convolution fusion | flops 1612447744 | bytes 4718592 | tf_op jit(solution)/shard_map/dot_general | solution.py:27
  77.9 21.3 %convolution_negate_fusion = f32[1024,128]{1,0:T(8,128)S(1)} fusion(f32[1024,1024]{0,1:T(8,128)S(1)} %fusion), kind=kOutput, calls=%fused_computation.14 | convolution fusion | flops 1612578816 | bytes 4718592 | tf_op jit(solution)/shard_map/dot_general | solution.py:27
  99.2 8.6 %gather_fusion = f32[1024,1024]{1,0:T(8,128)} fusion(f32[1024,1024]{0,1:T(8,128)} %get-tuple-element.7, s32[1024]{0:T(1024)S(1)} %get-tuple-element.29), kind=kCustom, calls=%fused_computation.clone | custom fusion | bytes 8392704 | tf_op jit(solution)/shard_map/jit(_take)/gather | solution.py:46
  107.8 8.6 %gather_fusion.1 = f32[1024,1024]{1,0:T(8,128)} fusion(f32[1024,1024]{0,1:T(8,128)} %get-tuple-element.7, s32[1024]{0:T(1024)S(1)} %get-tuple-element.30), kind=kCustom, calls=%fused_computation.1.clone | custom fusion | bytes 8392704 | tf_op jit(solution)/shard_map/jit(_take)/gather | solution.py:47
  116.4 4.0 %fusion.1 = f32[1024,1024]{0,1:T(8,128)S(1)} fusion(f32[1024,1024]{1,0:T(8,128)} %gather_fusion.1, f32[1024,1024]{1,0:T(8,128)} %gather_fusion, f32[1024]{0:T(1024)S(1)} %bitcast.250, f32[1024]{0:T(1024)S(1)} %bitcast.249, pred[1024]{0:T(1024)(128)(4,1)S(1)} %get-tuple-element.28, pred[1024]{0:T(1024)(128)(4,1)S(1)} %get-tuple-element.27), kind=kLoop, calls=%fused_computation.10 | loop fusion | flops 5242880 | bytes 12593152 | tf_op jit(solution)/shard_map/add | solution.py:48
  120.4 8.5 %fusion.34 = f32[1024,128]{1,0:T(8,128)S(1)} fusion(f32[1024,1024]{0,1:T(8,128)S(1)} %fusion.1), kind=kOutput, calls=%fused_computation.70 | convolution fusion | flops 1612447744 | bytes 4718592 | tf_op jit(solution)/shard_map/dot_general | solution.py:27
  128.9 8.9 %convolution_negate_fusion.1 = f32[1024,128]{1,0:T(8,128)S(1)} fusion(f32[1024,1024]{0,1:T(8,128)S(1)} %fusion.1), kind=kOutput, calls=%fused_computation.15 | convolution fusion | flops 1612578816 | bytes 4718592 | tf_op jit(solution)/shard_map/dot_general | solution.py:27
  137.9 3.0 fusion.42
  140.9 3.0 fusion.40
  143.9 3.0 fusion.3
  146.9 3.0 fusion.2
  149.9 3.0 fusion.46
  152.9 3.2 fusion.44
  156.1 3.0 fusion.5
  159.1 3.0 fusion.4
  168.7 47.5 %all-gather.3.cloned.1.call-done = f32[32,2,128,128]{3,2,1,0:T(8,128)} async-done(((f32[2,2,128,128]{3,2,1,0:T(8,128)}), f32[32,2,128,128]{3,2,1,0:T(8,128)}) %all-gather.3.cloned.1.call-update) | async-done | bytes 4194320 | tf_op jit(solution)/shard_map/all_gather | solution.py:113
  218.6 89.5 %all-reduce.4.cloned.1.call-done = (f32[2,128,128]{2,1,0:T(8,128)}, f32[2,128,128]{2,1,0:T(8,128)}) async-done(((f32[2,128,128]{2,1,0:T(8,128)}, f32[2,128,128]{2,1,0:T(8,128)}), (f32[2,128,128]{2,1,0:T(8,128)}, f32[2,128,128]{2,1,0:T(8,128)})) %all-reduce.4.cloned.1.call-update) | async-done | bytes 262160 | tf_op jit(solution)/shard_map/psum | solution.py:17
  319.8 32.4 %pmax.7 = f32[2]{0:T(128)} all-reduce(f32[2]{0:T(128)S(1)} %pad_maximum_fusion.2), channel_id=1, replica_groups=mesh['grp'=2,'slab'=16] {'slab'}, use_global_device_ids=true, to_apply=%region_9.11 | all-reduce | flops 2 | bytes 16 | tf_op jit(solution)/shard_map/pmax | solution.py:125
  (45 shorter events, 19.9 us)
Async XLA Ops:
  7.2 209.0 %all-gather.3.cloned.1.call-start = ((), (), s32[]{:S(2)}) async-start(), calls=%async_computation | async-start | bytes 4456448 | tf_op jit(solution)/shard_map/all_gather | solution.py:113
  56.4 8.6 %copy-start.1 = (f32[2,1024]{1,0:T(2,128)S(1)}, f32[2,1024]{1,0:T(2,128)}, u32[]{:S(2)}) copy-start(f32[2,1024]{1,0:T(2,128)} %param.14) | copy-start | bytes 24580
  152.9 10.0 %copy-start.3 = (s32[16]{0:T(128)S(1)}, s32[16]{0:T(128)}, u32[]{:S(2)}) copy-start(s32[16]{0:T(128)} %param.16) | copy-start | bytes 196
  152.9 11.9 %copy-start = (f32[1,2,128,128]{3,2,1,0:T(8,128)S(1)}, f32[1,2,128,128]{3,2,1,0:T(8,128)}, u32[]{:S(2)}) copy-start(f32[1,2,128,128]{3,2,1,0:T(8,128)} %param.17) | copy-start | bytes 393220
  152.9 12.7 %copy-start.2 = (s32[2,2]{1,0:T(2,128)S(1)}, s32[2,2]{1,0:T(2,128)}, u32[]{:S(2)}) copy-start(s32[2,2]{1,0:T(2,128)} %param.15) | copy-start | bytes 52
  162.8 145.3 %all-reduce.4.cloned.1.call-start = ((), (), s32[]{:S(2)}) async-start(), calls=%async_computation.1 | async-start | bytes 524288 | tf_op jit(solution)/shard_map/psum | solution.py:17
Sparse Core Ops, SparseCore 0:
  163.0 53.1 all-gather.2
  219.6 88.4 all-reduce.3
